TPU v7x, 32 devices: a whole 2x2x4 slice. The times are simulated.
32 devices in a mesh: wide: 8 (over z, x), group: 4 (over y, core).
Axes of the slice: x: 2, y: 2, z: 4, core: 2. Of those that a mesh axis runs over, the one named last changes fastest.
Arguments:
- feat4: bfloat16 [32, 24, 24, 256], P(('wide', 'group')), may hold values from -100 to 100
- feat5: bfloat16 [32, 12, 12, 256], P(('wide', 'group')), may hold values from -100 to 100
- feat6: bfloat16 [32, 6, 6, 256], P(('wide', 'group')), may hold values from -100 to 100
- feat7: bfloat16 [32, 3, 3, 256], P(('wide', 'group')), may hold values from -100 to 100
- out_grad4: bfloat16 [32, 24, 24, 256], P(('wide', 'group')), may hold values from -6 to 6
- out_grad5: bfloat16 [32, 12, 12, 256], P(('wide', 'group')), may hold values from -6 to 6
- out_grad6: bfloat16 [32, 6, 6, 256], P(('wide', 'group')), may hold values from -6 to 6
- out_grad7: bfloat16 [32, 3, 3, 256], P(('wide', 'group')), may hold values from -6 to 6
- conv_weight: bfloat16 [3, 3, 256, 256], replicated, may hold values from -0.125 to 0.125
- bn_gain: float32 [4, 256], replicated, may hold values from 0.25 to 1.75
- bn_shift: float32 [4, 256], replicated, may hold values from -0.5 to 0.5
- heights: int32 [32], P(('wide', 'group')), may hold values from 168 to 384
- widths: int32 [32], P(('wide', 'group')), may hold values from 168 to 384
Outputs:
- out4: bfloat16 [32, 24, 24, 256], P(('wide', 'group'))
- out5: bfloat16 [32, 12, 12, 256], P(('wide', 'group'))
- out6: bfloat16 [32, 6, 6, 256], P(('wide', 'group'))
- out7: bfloat16 [32, 3, 3, 256], P(('wide', 'group'))
- d_feat4: bfloat16 [32, 24, 24, 256], P(('wide', 'group'))
- d_feat5: bfloat16 [32, 12, 12, 256], P(('wide', 'group'))
- d_feat6: bfloat16 [32, 6, 6, 256], P(('wide', 'group'))
- d_feat7: bfloat16 [32, 3, 3, 256], P(('wide', 'group'))
- d_weight: float32 [3, 3, 256, 256], replicated
- d_gain: float32 [4, 256], replicated
- d_shift: float32 [4, 256], replicated
Inputs may be any that keep to these rules, and one draw needn't show every extreme that they name: `heights`: pixel height of the valid part of each image. `widths`: pixel width of the valid part of each image.
All inputs are finite; a program needn't handle non-finite values.
Results may differ from a plain program's by a relative error of at most 0.0049.
Values sent between devices are 32-bit elements; how exact they have to be, the bound alone decides.
A program may use at most 64 MiB of HBM per device.

v0:
```python
import jax
import jax.numpy as jnp
from jax import lax
from jax.sharding import PartitionSpec as P

EPSILON = 1e-05


def level_mask(heights, widths, stride, extent):
    row_limit = (heights[0] + stride - 1) // stride
    col_limit = (widths[0] + stride - 1) // stride
    row_place = lax.broadcasted_iota(jnp.int32, (extent, extent), 0)
    col_place = lax.broadcasted_iota(jnp.int32, (extent, extent), 1)
    inside = jnp.logical_and(row_place < row_limit, col_place < col_limit)
    return (inside.astype(jnp.float32), row_limit)


def conv_rows(padded, conv_weight, start_row, row_count, extent):
    summed = jnp.zeros((row_count * extent, conv_weight.shape[3]), jnp.float32)
    for tap_row in range(3):
        for tap_col in range(3):
            window = lax.dynamic_slice_in_dim(padded, start_row + tap_row, row_count, 0)[
                :, tap_col : tap_col + extent, :
            ]
            summed = summed + jnp.dot(
                window.reshape(row_count * extent, -1),
                conv_weight[tap_row, tap_col],
                preferred_element_type=jnp.float32,
            )
    return summed.reshape(row_count, extent, -1)


def input_grad_rows(padded_back, conv_weight, start_row, row_count, extent):
    summed = jnp.zeros((row_count * extent, conv_weight.shape[2]), jnp.float32)
    for tap_row in range(3):
        for tap_col in range(3):
            window = lax.dynamic_slice_in_dim(padded_back, start_row + 2 - tap_row, row_count, 0)[
                :, 2 - tap_col : 2 - tap_col + extent, :
            ]
            summed = summed + lax.dot_general(
                window.reshape(row_count * extent, -1),
                conv_weight[tap_row, tap_col],
                (((1,), (1,)), ((), ())),
                preferred_element_type=jnp.float32,
            )
    return summed.reshape(row_count, extent, -1)


def weight_grad_rows(padded, back_rows, start_row, row_count, extent):
    flat_back = back_rows.reshape(row_count * extent, -1)
    tap_terms = []
    for tap_row in range(3):
        for tap_col in range(3):
            window = lax.dynamic_slice_in_dim(padded, start_row + tap_row, row_count, 0)[
                :, tap_col : tap_col + extent, :
            ]
            tap_terms.append(
                lax.dot_general(
                    window.reshape(row_count * extent, -1),
                    flat_back,
                    (((0,), (0,)), ((), ())),
                    preferred_element_type=jnp.float32,
                )
            )
    return jnp.stack(tap_terms).reshape(3, 3, padded.shape[2], flat_back.shape[1])


def forward_conv(padded, conv_weight, extent):
    conv_out = conv_rows(padded, conv_weight, 0, extent, extent)
    return conv_out


def backward_conv(padded, back_grad, conv_weight, extent):
    padded_back = jnp.pad(back_grad, ((1, 1), (1, 1), (0, 0)))
    weight_part = weight_grad_rows(padded, back_grad, 0, extent, extent)
    input_part = input_grad_rows(padded_back, conv_weight, 0, extent, extent)
    return (weight_part, input_part)


def combine_stats(values):
    within = lax.psum(values, "group")
    result = lax.psum(within, "wide")
    return result


def combine_grads(values):
    within = lax.psum(values, "group")
    result = lax.psum(within, "wide")
    return result


def shards(
    feat4,
    feat5,
    feat6,
    feat7,
    out_grad4,
    out_grad5,
    out_grad6,
    out_grad7,
    conv_weight,
    bn_gain,
    bn_shift,
    heights,
    widths,
):
    features = (feat4, feat5, feat6, feat7)
    cotangents = (out_grad4, out_grad5, out_grad6, out_grad7)
    devices = lax.axis_size("wide") * lax.axis_size("group")
    levels = []
    for level_index in range(4):
        feature = features[level_index][0]
        extent = feature.shape[0]
        valid_mask, row_limit = level_mask(heights, widths, 16 * 2**level_index, extent)
        weighted = valid_mask[:, :, None]
        padded = jnp.pad(feature * weighted.astype(feature.dtype), ((1, 1), (1, 1), (0, 0)))
        conv_out = forward_conv(padded, conv_weight, extent)
        levels.append((valid_mask, row_limit, weighted, padded, conv_out))
    moments = []
    local_sums = jnp.stack(
        [jnp.sum(level_entry[4] * level_entry[2], axis=(0, 1)) for level_entry in levels]
    )
    local_squares = jnp.stack(
        [
            jnp.sum(level_entry[2] * level_entry[4] * level_entry[4], axis=(0, 1))
            for level_entry in levels
        ]
    )
    local_counts = jnp.stack([jnp.sum(level_entry[0]) for level_entry in levels])
    moment_sums, squares, counts = combine_stats((local_sums, local_squares, local_counts))
    for level_index in range(4):
        pixel_count = counts[level_index]
        mean_value = moment_sums[level_index] / pixel_count
        moments.append(
            (pixel_count, mean_value, squares[level_index] / pixel_count - mean_value * mean_value)
        )
    finals = []
    for level_index in range(4):
        valid_mask, row_limit, weighted, padded, conv_out = levels[level_index]
        pixel_count, mean_value, variance = moments[level_index]
        inverse = lax.rsqrt(variance + EPSILON)
        normed = (conv_out - mean_value) * inverse
        shifted = bn_gain[level_index] * normed + bn_shift[level_index]
        sigmoid_value = jax.nn.sigmoid(shifted)
        output = (weighted * shifted * sigmoid_value).astype(jnp.bfloat16)
        slope_term = (
            weighted
            * cotangents[level_index][0].astype(jnp.float32)
            * sigmoid_value
            * (1.0 + shifted * (1.0 - sigmoid_value))
        )
        finals.append((output, normed, inverse, slope_term))
    shift_local = jnp.stack([jnp.sum(final_entry[3], axis=(0, 1)) for final_entry in finals])
    gain_local = jnp.stack(
        [jnp.sum(final_entry[3] * final_entry[1], axis=(0, 1)) for final_entry in finals]
    )
    shift_rows, gain_rows = combine_stats((shift_local, gain_local))
    back_sums = [(shift_rows[level_index], gain_rows[level_index]) for level_index in range(4)]
    weight_local = jnp.zeros(conv_weight.shape, jnp.float32)
    outputs = []
    input_grads = []
    shift_list = []
    gain_list = []
    for level_index in range(4):
        valid_mask, row_limit, weighted, padded, conv_out = levels[level_index]
        pixel_count, mean_value, variance = moments[level_index]
        output, normed, inverse, slope_term = finals[level_index]
        shift_sum, gain_sum = back_sums[level_index]
        extent = conv_out.shape[0]
        back_grad = (
            weighted
            * (bn_gain[level_index] * inverse)
            * (slope_term - shift_sum / pixel_count - normed * (gain_sum / pixel_count))
        ).astype(jnp.bfloat16)
        weight_part, input_part = backward_conv(padded, back_grad, conv_weight, extent)
        weight_local = weight_local + weight_part
        input_grads.append((weighted * input_part).astype(jnp.bfloat16)[None])
        outputs.append(output[None])
        shift_list.append(shift_sum)
        gain_list.append(gain_sum)
    weight_total = combine_grads(weight_local)
    return (
        outputs[0],
        outputs[1],
        outputs[2],
        outputs[3],
        input_grads[0],
        input_grads[1],
        input_grads[2],
        input_grads[3],
        weight_total / devices,
        jnp.stack(gain_list) / devices,
        jnp.stack(shift_list) / devices,
    )


def solution(mesh):
    placed = (
        P(("wide", "group"), None, None, None),
        P(("wide", "group"), None, None, None),
        P(("wide", "group"), None, None, None),
        P(("wide", "group"), None, None, None),
        P(("wide", "group"), None, None, None),
        P(("wide", "group"), None, None, None),
        P(("wide", "group"), None, None, None),
        P(("wide", "group"), None, None, None),
        P(),
        P(),
        P(),
        P(("wide", "group")),
        P(("wide", "group")),
    )
    return jax.shard_map(
        shards,
        mesh=mesh,
        in_specs=placed,
        out_specs=(
            P(("wide", "group"), None, None, None),
            P(("wide", "group"), None, None, None),
            P(("wide", "group"), None, None, None),
            P(("wide", "group"), None, None, None),
            P(("wide", "group"), None, None, None),
            P(("wide", "group"), None, None, None),
            P(("wide", "group"), None, None, None),
            P(("wide", "group"), None, None, None),
            P(),
            P(),
            P(),
        ),
        check_vma=False,
    )
```

profile of v0, /device:TPU:0, one launch (start us, length us, event | category | flops | bytes accessed | tf_op | source)
XLA Modules:
  0.0 299.1 jit_solution(16657673691624110499)
XLA Ops:
  18.4 1.1 convolution_add_fusion.63
  19.4 1.1 convolution_add_fusion.62
  35.5 2.6 pad_maximum_fusion.4
  38.2 8.7 %all-reduce.11 = (f32[4,256]{1,0:T(4,128)S(1)}, f32[4]{0:T(128)S(1)}, f32[4,256]{1,0:T(4,128)S(1)}) all-reduce(f32[4,256]{1,0:T(4,128)S(1)} %pad_maximum_fusion.1, f32[4]{0:T(128)S(1)} %pad_maximum_fusion.4, f32[4,256]{1,0:T(4,128)S(1)} %pad_maximum_fusion), channel_id=1, replica_groups=mesh['wide'=8,'group'=4] {'group'}, use_global_device_ids=true, to_apply=%region_16.17 | all-reduce | flops 2052 | bytes 16416 | tf_op jit(solution)/shard_map/psum | solution.py:81
  46.9 22.2 %all-reduce.9 = (f32[4,256]{1,0:T(4,128)S(1)}, f32[4]{0:T(128)S(1)}, f32[4,256]{1,0:T(4,128)S(1)}) all-reduce(f32[4,256]{1,0:T(4,128)S(1)} %get-tuple-element.34, f32[4]{0:T(128)S(1)} %get-tuple-element.35, f32[4,256]{1,0:T(4,128)S(1)} %get-tuple-element.36), channel_id=1, replica_groups=mesh['wide'=8,'group'=4] {'wide'}, use_global_device_ids=true, to_apply=%region_17.18 | all-reduce | flops 2052 | bytes 16416 | tf_op jit(solution)/shard_map/psum | solution.py:82
  69.7 2.6 slice_divide_fusion.8
  72.3 2.6 slice_divide_fusion.9
  78.9 5.9 %all-reduce.10 = (f32[4,256]{1,0:T(4,128)S(1)}, f32[4,256]{1,0:T(4,128)S(1)}) all-reduce(f32[4,256]{1,0:T(4,128)S(1)} %pad_maximum_fusion.3, f32[4,256]{1,0:T(4,128)S(1)} %pad_maximum_fusion.2), channel_id=1, replica_groups=mesh['wide'=8,'group'=4] {'group'}, use_global_device_ids=true, to_apply=%region_28.29 | all-reduce | flops 2048 | bytes 16384 | tf_op jit(solution)/shard_map/psum | solution.py:81
  84.8 17.6 %all-reduce.8 = (f32[4,256]{1,0:T(4,128)S(1)}, f32[4,256]{1,0:T(4,128)S(1)}) all-reduce(f32[4,256]{1,0:T(4,128)S(1)} %get-tuple-element.32, f32[4,256]{1,0:T(4,128)S(1)} %get-tuple-element.33), channel_id=1, replica_groups=mesh['wide'=8,'group'=4] {'wide'}, use_global_device_ids=true, to_apply=%region_29.30 | all-reduce | flops 2048 | bytes 16384 | tf_op jit(solution)/shard_map/psum | solution.py:82
  102.4 2.6 slice_divide_fusion
  105.1 2.6 slice_divide_fusion.1
  107.9 1.1 multiply_convert_fusion.2
  120.9 2.1 add_add_fusion
  127.0 1.3 reshape.1156
  128.3 1.3 reshape.1150
  129.6 1.3 reshape.1151
  130.9 1.3 reshape.1152
  132.2 1.3 reshape.1153
  140.1 1.4 multiply_convert_fusion.21
  153.2 1.2 pad_slice_fusion
  156.1 20.6 %all-reduce.15.cloned.1.call-done = f32[3,3,256,256]{3,2,1,0:T(8,128)} async-done(((f32[3,3,256,256]{3,2,1,0:T(8,128)}), f32[3,3,256,256]{3,2,1,0:T(8,128)}) %all-reduce.15.cloned.1.call-update) | async-done | bytes 2359312 | tf_op jit(solution)/shard_map/psum | solution.py:87
  176.7 1.9 multiply_convert_fusion.6
  182.7 106.2 %all-reduce.17.cloned.1.call-done = f32[3,3,256,256]{3,2,1,0:T(8,128)} async-done(((f32[3,3,256,256]{3,2,1,0:T(8,128)}), f32[3,3,256,256]{3,2,1,0:T(8,128)}) %all-reduce.17.cloned.1.call-update) | async-done | bytes 2359312 | tf_op jit(solution)/shard_map/psum | solution.py:88
  289.0 3.3 %broadcast_multiply_fusion = f32[3,3,256,256]{3,2,1,0:T(8,128)} fusion(f32[3,3,256,256]{3,2,1,0:T(8,128)} %all-reduce.17.cloned.1.call-done), kind=kLoop, calls=%fused_computation.17 | loop fusion | flops 589824 | bytes 4718592 | tf_op jit(solution)/shard_map/div | solution.py:191
  (500 shorter events, 67.1 us)
Async XLA Ops:
  7.2 169.5 %all-reduce.15.cloned.1.call-start = ((), (), s32[]{:S(2)}) async-start(), calls=%async_computation | async-start | bytes 4718592 | tf_op jit(solution)/shard_map/psum | solution.py:87
  32.2 45.2 %copy-start.45 = (f32[1,256]{1,0:T(1,128)}, f32[1,256]{1,0:T(1,128)S(1)}, u32[]{:S(2)}) copy-start(f32[1,256]{1,0:T(1,128)S(1)} %get-tuple-element.118) | copy-start | bytes 3076
  32.2 45.6 %copy-start.66 = (f32[1,256]{1,0:T(1,128)}, f32[1,256]{1,0:T(1,128)S(1)}, u32[]{:S(2)}) copy-start(f32[1,256]{1,0:T(1,128)S(1)} %get-tuple-element.117) | copy-start | bytes 3076
  32.2 45.7 %copy-start.69 = (f32[1,256]{1,0:T(1,128)}, f32[1,256]{1,0:T(1,128)S(1)}, u32[]{:S(2)}) copy-start(f32[1,256]{1,0:T(1,128)S(1)} %get-tuple-element.119) | copy-start | bytes 3076
  32.2 45.9 %copy-start.98 = (f32[1,256]{1,0:T(1,128)}, f32[1,256]{1,0:T(1,128)S(1)}, u32[]{:S(2)}) copy-start(f32[1,256]{1,0:T(1,128)S(1)} %get-tuple-element.116) | copy-start | bytes 3076
  32.3 45.1 %copy-start.56 = (f32[1,256]{1,0:T(1,128)}, f32[1,256]{1,0:T(1,128)S(1)}, u32[]{:S(2)}) copy-start(f32[1,256]{1,0:T(1,128)S(1)} %get-tuple-element.130) | copy-start | bytes 3076
  32.3 45.5 %copy-start.84 = (f32[1,256]{1,0:T(1,128)}, f32[1,256]{1,0:T(1,128)S(1)}, u32[]{:S(2)}) copy-start(f32[1,256]{1,0:T(1,128)S(1)} %get-tuple-element.129) | copy-start | bytes 3076
  32.3 45.7 %copy-start.87 = (f32[1,256]{1,0:T(1,128)}, f32[1,256]{1,0:T(1,128)S(1)}, u32[]{:S(2)}) copy-start(f32[1,256]{1,0:T(1,128)S(1)} %get-tuple-element.131) | copy-start | bytes 3076
  32.3 45.8 %copy-start.100 = (f32[1,256]{1,0:T(1,128)}, f32[1,256]{1,0:T(1,128)S(1)}, u32[]{:S(2)}) copy-start(f32[1,256]{1,0:T(1,128)S(1)} %get-tuple-element.128) | copy-start | bytes 3076
  34.6 42.8 %copy-start.1 = (bf16[1,24,24,256]{3,2,1,0:T(8,128)(2,1)S(1)}, bf16[1,24,24,256]{3,2,1,0:T(8,128)(2,1)}, u32[]{:S(2)}) copy-start(bf16[1,24,24,256]{3,2,1,0:T(8,128)(2,1)} %param.17) | copy-start | bytes 884740
  34.6 42.8 %copy-start.18 = (f32[24,24]{1,0:T(8,128)S(1)}, f32[24,24]{1,0:T(8,128)}, u32[]{:S(2)}) copy-start(f32[24,24]{1,0:T(8,128)} %get-tuple-element.150) | copy-start | bytes 6916
  35.2 42.6 %copy-start.7 = (bf16[1,12,12,256]{3,2,1,0:T(8,128)(2,1)S(1)}, bf16[1,12,12,256]{3,2,1,0:T(8,128)(2,1)}, u32[]{:S(2)}) copy-start(bf16[1,12,12,256]{3,2,1,0:T(8,128)(2,1)} %param.18) | copy-start | bytes 221188
  35.2 42.8 %copy-start.16 = (bf16[1,6,6,256]{3,2,1,0:T(8,128)(2,1)S(1)}, bf16[1,6,6,256]{3,2,1,0:T(8,128)(2,1)}, u32[]{:S(2)}) copy-start(bf16[1,6,6,256]{3,2,1,0:T(8,128)(2,1)} %param.19) | copy-start | bytes 55300
  35.2 42.8 %copy-start.37 = (f32[6,6]{1,0:T(8,128)S(1)}, f32[6,6]{1,0:T(8,128)}, u32[]{:S(2)}) copy-start(f32[6,6]{1,0:T(8,128)} %get-tuple-element.146) | copy-start | bytes 436
  35.2 43.0 %copy-start.26 = (f32[3,3,256]{2,1,0:T(4,128)S(1)}, f32[3,3,256]{2,1,0:T(4,128)}, u32[]{:S(2)}) copy-start(f32[3,3,256]{2,1,0:T(4,128)} %reshape.1121) | copy-start | bytes 27652
  35.2 43.0 %copy-start.48 = (f32[3,3]{1,0:T(4,128)S(1)}, f32[3,3]{1,0:T(4,128)}, u32[]{:S(2)}) copy-start(f32[3,3]{1,0:T(4,128)} %get-tuple-element.144) | copy-start | bytes 112
  35.2 43.0 %copy-start.74 = (bf16[1,3,3,256]{3,2,1,0:T(4,128)(2,1)S(1)}, bf16[1,3,3,256]{3,2,1,0:T(4,128)(2,1)}, u32[]{:S(2)}) copy-start(bf16[1,3,3,256]{3,2,1,0:T(4,128)(2,1)} %param.20) | copy-start | bytes 13828
  75.0 32.8 %copy-start.42 = (f32[1,256]{1,0:T(1,128)}, f32[1,256]{1,0:T(1,128)S(1)}, u32[]{:S(2)}) copy-start(f32[1,256]{1,0:T(1,128)S(1)} %get-tuple-element.123) | copy-start | bytes 3076
  75.0 32.8 %copy-start.60 = (f32[1,256]{1,0:T(1,128)}, f32[1,256]{1,0:T(1,128)S(1)}, u32[]{:S(2)}) copy-start(f32[1,256]{1,0:T(1,128)S(1)} %get-tuple-element.122) | copy-start | bytes 3076
  75.0 32.8 %copy-start.63 = (f32[1,256]{1,0:T(1,128)}, f32[1,256]{1,0:T(1,128)S(1)}, u32[]{:S(2)}) copy-start(f32[1,256]{1,0:T(1,128)S(1)} %get-tuple-element.121) | copy-start | bytes 3076
  75.0 32.8 %copy-start.72 = (f32[1,256]{1,0:T(1,128)}, f32[1,256]{1,0:T(1,128)S(1)}, u32[]{:S(2)}) copy-start(f32[1,256]{1,0:T(1,128)S(1)} %get-tuple-element.120) | copy-start | bytes 3076
  75.6 32.2 %copy-start.81 = (f32[256]{0:T(256)}, f32[256]{0:T(256)S(1)}, u32[]{:S(2)}) copy-start(f32[256]{0:T(256)S(1)} %get-tuple-element.137) | copy-start | bytes 3076
  76.2 31.6 %copy-start.92 = (f32[256]{0:T(256)}, f32[256]{0:T(256)S(1)}, u32[]{:S(2)}) copy-start(f32[256]{0:T(256)S(1)} %get-tuple-element.135) | copy-start | bytes 3076
  123.0 165.9 %all-reduce.17.cloned.1.call-start = ((), (), s32[]{:S(2)}) async-start(), calls=%async_computation.1 | async-start | bytes 4718592 | tf_op jit(solution)/shard_map/psum | solution.py:88
  (105 other events, 406.5 us)
Sparse Core Ops, SparseCore 0:
  123.2 53.5 all-reduce.14
  180.3 108.6 all-reduce.16
where the time goes:
time: 301 us; the launch traced here: 299 us
  waiting for transfers between devices  127 us (42%)
  blocking collectives  54.4 us (18%)
  other arithmetic  41.2 us (14%)
  matrix products  34 us (11%)
  local copies, waits for them, and re-layouts  24.6 us (8%)
  between operations  18.1 us (6%)
    psum x1, waiting for transfers between devices, combine_grads(): result = lax.psum(within, 'wide')  106 us
    psum x2, blocking collectives, combine_stats(): result = lax.psum(within, 'wide')  39.7 us
    psum x1, waiting for transfers between devices, combine_grads(): within = lax.psum(values, 'group')  20.6 us
    psum x2, blocking collectives, combine_stats(): within = lax.psum(values, 'group')  14.6 us
    dot_general x36, matrix products, input_grad_rows(): lax.dot_general(window.reshape(row_count * extent, -1), conv_weight[tap_r...  14.1 us
    reshape x24, local copies, waits for them, and re-layouts, input_grad_rows(): window.reshape(row_count * extent, -1)  11.1 us
    dot_general x36, matrix products, conv_rows(): jnp.dot(window.reshape(row_count * extent, -1), conv_weight[tap_row, tap_...  10.4 us
    dot_general x36, matrix products, weight_grad_rows(): lax.dot_general(window.reshape(row_count * extent, -1), flat_back, (((0,)...  9.51 us
  transfers between devices with their start and end apart: 2, of which 2 were waited for; matrix products, arithmetic and copies ran while one was open for 12% of the time, Pallas kernels for 0%

commit v1 on v0

v1 whole, which is shorter than its diff:
```python
import functools
import math

import jax
import jax.numpy as jnp
from jax import lax
from jax.experimental import pallas as pl
from jax.experimental.pallas import tpu as pltpu
from jax.sharding import PartitionSpec as P

EPSILON = 1e-05
MESH = pl.DeviceIdType.MESH
TILE = 48


def plan(extents):
    segments = []
    for index, extent in enumerate(extents):
        pitch = -(-(extent + 1) // 16) * 16
        if segments and segments[-1]["pitch"] == pitch:
            segments[-1]["levels"].append(index)
        else:
            segments.append({"pitch": pitch, "levels": [index]})
    base = 0
    places = {}
    for number, segment in enumerate(segments):
        pitch = segment["pitch"]
        at = 0
        holes = [(0, pitch)]
        for index in segment["levels"]:
            size = extents[index] * pitch
            places[index] = (number, at, size, pitch)
            holes.append((pitch + at + size, pitch))
            at += size + pitch
        rows = -(-(at - pitch) // 128) * 128
        last = holes.pop()
        holes.append((last[0], rows + 2 * pitch - last[0]))
        segment.update(rows=rows, base=base, holes=holes)
        base += rows
    return segments, places, base


class Hop:
    def __init__(self, size, place, target):
        self.size, self.place, self.target = size, place, target


def kernel(shape, *refs):
    names = shape["names"]
    ref = dict(zip(names, refs))
    extents, wide, group = shape["extents"], shape["wide"], shape["group"]
    segments, places, total_rows = plan(extents)
    levels = len(extents)
    ch = shape["ch"]
    w_me, g_me = lax.axis_index("wide"), lax.axis_index("group")
    x_size, y_size, z_size = shape["x"], shape["y"], shape["z"]
    devices = wide * group

    def at_group(g):
        return {"wide": w_me, "group": g}

    def at_wide(w):
        return {"wide": w, "group": g_me}

    barrier = pltpu.get_barrier_semaphore()
    for step in range(1, group):
        pl.semaphore_signal(barrier, inc=1, device_id=at_group(lax.rem(g_me + step, group)), device_id_type=MESH)
    for step in range(1, wide):
        pl.semaphore_signal(barrier, inc=1, device_id=at_wide(lax.rem(w_me + step, wide)), device_id_type=MESH)

    height, width = ref["heights"][0], ref["widths"][0]
    row_limits, col_limits = [], []
    for index in range(levels):
        stride = 16 * 2**index
        row_limits.append(jnp.minimum((height + (stride - 1)) // stride, extents[index]))
        col_limits.append(jnp.minimum((width + (stride - 1)) // stride, extents[index]))

    masks, conv = ref["masks"], ref["conv"]
    xbs = [ref[f"xb{n}"] for n in range(len(segments))]
    bbs = [ref[f"bb{n}"] for n in range(len(segments))]
    for number, segment in enumerate(segments):
        for start, count in segment["holes"]:
            xbs[number][start : start + count, :] = jnp.zeros((count, 3 * ch), jnp.bfloat16)
            bbs[number][start : start + count, :] = jnp.zeros((count, 3 * ch), jnp.bfloat16)

    def spread(target, index, values):
        number, at, size, pitch = places[index]
        rows = slice(pitch + at, pitch + at + size)
        target[number][rows, 0:ch] = pltpu.roll(values, 1, 0).astype(jnp.bfloat16)
        target[number][rows, ch : 2 * ch] = values.astype(jnp.bfloat16)
        target[number][rows, 2 * ch : 3 * ch] = pltpu.roll(values, size - 1, 0).astype(jnp.bfloat16)

    def span(index):
        number, at, size, pitch = places[index]
        start = segments[number]["base"] + at
        return start, size

    for index in range(levels):
        number, at, size, pitch = places[index]
        start, _ = span(index)
        extent = extents[index]
        spot = lax.broadcasted_iota(jnp.int32, (extent, pitch, ch), 1)
        line = lax.broadcasted_iota(jnp.int32, (extent, pitch, ch), 0)
        inside = jnp.logical_and(line < row_limits[index], spot < col_limits[index])
        mask = jnp.where(inside, 1.0, 0.0).reshape(size, ch)
        masks[start : start + size, :] = mask
        stage = ref[f"stage{index}"]
        stage[...] = jnp.zeros(stage.shape, jnp.float32)
        stage[:, 0:extent, :] = ref[f"feat{index}"][0].astype(jnp.float32)
        spread(xbs, index, stage[...].reshape(size, ch) * mask)

    weight = ref["weight"]
    sums = ref["sums1"]

    def fold(values):
        return jnp.sum(values.reshape(-1, 8, ch), axis=0)

    for number, segment in enumerate(segments):
        rows, pitch, base = segment["rows"], segment["pitch"], segment["base"]
        total = None
        for tap in range(3):
            part = jnp.dot(
                xbs[number][tap * pitch : tap * pitch + rows, :],
                weight[tap].reshape(3 * ch, ch),
                preferred_element_type=jnp.float32,
            )
            total = part if total is None else total + part
        conv[base : base + rows, :] = total
    for index in range(levels):
        start, size = span(index)
        total = jnp.zeros((8, ch), jnp.float32)
        square = jnp.zeros((8, ch), jnp.float32)
        for row in range(start, start + size, TILE):
            values = conv[row : row + TILE, :]
            masked = values * masks[row : row + TILE, :]
            total += fold(masked)
            square += fold(masked * values)
        sums[index : index + 1, 0:ch] = jnp.sum(total, axis=0, keepdims=True)
        sums[levels + index : levels + index + 1, 0:ch] = jnp.sum(square, axis=0, keepdims=True)
        cells = (row_limits[index] * col_limits[index]).astype(jnp.float32)
        for row in (index, levels + index):
            sums[row : row + 1, ch : ch + 128] = jnp.full((1, 128), cells, jnp.float32)

    pl.semaphore_wait(barrier, group - 1 + wide - 1)

    def exchange(tag, during):
        sent, first, held, second = ref["sums" + tag], ref["near" + tag], ref["held" + tag], ref["far" + tag]
        copies = []
        for step in range(1, group):
            copies.append(
                pltpu.make_async_remote_copy(
                    src_ref=sent,
                    dst_ref=first.at[g_me],
                    send_sem=ref["near_send" + tag].at[step - 1],
                    recv_sem=ref["near_recv" + tag].at[step - 1],
                    device_id=at_group(lax.rem(g_me + step, group)),
                    device_id_type=MESH,
                )
            )
            copies[-1].start()
        during[0]()
        own = sent[...]
        for copy in copies:
            copy.wait()
        total = None
        for source in range(group):
            term = jnp.where(source == g_me, own, first[source])
            total = term if total is None else total + term
        held[...] = total
        copies = []
        for step in range(1, wide):
            copies.append(
                pltpu.make_async_remote_copy(
                    src_ref=held,
                    dst_ref=second.at[w_me],
                    send_sem=ref["far_send" + tag].at[step - 1],
                    recv_sem=ref["far_recv" + tag].at[step - 1],
                    device_id=at_wide(lax.rem(w_me + step, wide)),
                    device_id_type=MESH,
                )
            )
            copies[-1].start()
        during[1]()
        own = held[...]
        for copy in copies:
            copy.wait()
        total = None
        for source in range(wide):
            term = jnp.where(source == w_me, own, second[source])
            total = term if total is None else total + term
        return total

    grads = ref["grads"]

    def take_grads():
        for index in range(levels):
            start, size = span(index)
            extent = extents[index]
            stage = ref[f"stage{index}"]
            stage[:, 0:extent, :] = ref[f"grad{index}"][0].astype(jnp.float32)
            grads[start : start + size, :] = stage[...].reshape(size, ch) * masks[start : start + size, :]

    def turn():
        for number, segment in enumerate(segments):
            rows, pitch, base = segment["rows"], segment["pitch"], segment["base"]
            for row in range(0, rows, 128):
                block = xbs[number][pitch + row : pitch + row + 128, ch : 2 * ch]
                ref["turned"][:, base + row : base + row + 128] = block.astype(jnp.float32).T.astype(jnp.bfloat16)

    moments = exchange("1", (take_grads, turn))

    sums = ref["sums2"]
    scales, counts = [], []
    for index in range(levels):
        start, size = span(index)
        count = jnp.concatenate([moments[index : index + 1, ch : ch + 128]] * (ch // 128), axis=1)
        mean = moments[index : index + 1, 0:ch] / count
        variance = jnp.maximum(moments[levels + index : levels + index + 1, 0:ch] / count - mean * mean, 0.0)
        inverse = lax.rsqrt(variance + EPSILON)
        gain = ref["gain"][index : index + 1, :]
        shift = ref["shift"][index : index + 1, :]
        counts.append(count)
        scales.append(gain * inverse)
        shift_sum = jnp.zeros((8, ch), jnp.float32)
        gain_sum = jnp.zeros((8, ch), jnp.float32)
        for row in range(start, start + size, TILE):
            normed = (conv[row : row + TILE, :] - mean) * inverse
            shifted = gain * normed + shift
            sigma = 1.0 / (1.0 + jnp.exp(-shifted))
            slope = grads[row : row + TILE, :] * sigma * (1.0 + shifted * (1.0 - sigma))
            conv[row : row + TILE, :] = normed
            grads[row : row + TILE, :] = slope
            ref["acts"][row : row + TILE, :] = masks[row : row + TILE, :] * shifted * sigma
            shift_sum += fold(slope)
            gain_sum += fold(slope * normed)
        sums[index : index + 1, :] = jnp.sum(shift_sum, axis=0, keepdims=True)
        sums[levels + index : levels + index + 1, :] = jnp.sum(gain_sum, axis=0, keepdims=True)

    def put_acts():
        for index in range(levels):
            start, size = span(index)
            extent, pitch = extents[index], places[index][3]
            values = ref["acts"][start : start + size, :].reshape(extent, pitch, ch)
            ref[f"out{index}"][0] = values[:, 0:extent, :].astype(jnp.bfloat16)

    slopes = exchange("2", (lambda: None, put_acts))
    ref["d_shift"][...] = slopes[0:levels, :] / devices
    ref["d_gain"][...] = slopes[levels : 2 * levels, :] / devices

    for index in range(levels):
        start, size = span(index)
        shift_term = slopes[index : index + 1, :] / counts[index]
        gain_term = slopes[levels + index : levels + index + 1, :] / counts[index]
        for row in range(start, start + size, TILE):
            grads[row : row + TILE, :] = (
                masks[row : row + TILE, :]
                * scales[index]
                * (grads[row : row + TILE, :] - shift_term - conv[row : row + TILE, :] * gain_term)
            )
        spread(bbs, index, grads[start : start + size, :])

    def weight_grad(tap):
        a, b = divmod(tap, 3)
        total = None
        for number, segment in enumerate(segments):
            rows, pitch, base = segment["rows"], segment["pitch"], segment["base"]
            part = jnp.dot(
                ref["turned"][:, base : base + rows],
                bbs[number][(2 - a) * pitch : (2 - a) * pitch + rows, (2 - b) * ch : (3 - b) * ch],
                preferred_element_type=jnp.float32,
            )
            total = part if total is None else total + part
        return total

    def input_grad(number, begin, count):
        pitch, base = segments[number]["pitch"], segments[number]["base"]
        total = None
        for a in range(3):
            for b in range(3):
                first = (2 - a) * pitch + begin
                part = lax.dot_general(
                    bbs[number][first : first + count, (2 - b) * ch : (3 - b) * ch],
                    weight[a, b],
                    (((1,), (1,)), ((), ())),
                    preferred_element_type=jnp.float32,
                )
                total = part if total is None else total + part
        where = slice(base + begin, base + begin + count)
        ref["acts"][where, :] = total * masks[where, :]

    def put_input_grads():
        for index in range(levels):
            start, size = span(index)
            extent, pitch = extents[index], places[index][3]
            values = ref["acts"][start : start + size, :].reshape(extent, pitch, ch)
            ref[f"d_feat{index}"][0] = values[:, 0:extent, :].astype(jnp.bfloat16)

    jobs = []
    for number, segment in enumerate(segments):
        tall = 256 if segment["rows"] % 256 == 0 else segment["rows"]
        for begin in range(0, segment["rows"], tall):
            jobs.append(functools.partial(input_grad, number, begin, tall))
    jobs.append(put_input_grads)

    if not shape["fused"]:
        for tap in range(9):
            ref["d_weight"][tap] = weight_grad(tap)
        for job in jobs:
            job()
        return

    part_ref, whole = ref["parts"], ref["d_weight"]
    core, y_me = lax.rem(g_me, 2), g_me // 2
    z_me, x_me = w_me // x_size, lax.rem(w_me, x_size)
    hops = {
        "core": Hop(2, core, lambda k: at_group(y_me * 2 + k)),
        "y": Hop(y_size, y_me, lambda k: at_group(k * 2 + core)),
        "x": Hop(x_size, x_me, lambda k: at_wide(z_me * x_size + k)),
        "z": Hop(z_size, z_me, lambda k: at_wide(k * x_size + x_me)),
    }

    class Chunk:
        def __init__(self, tap):
            self.tap = tap
            order = ("core", "x", "y", "z") if tap % 2 == 0 else ("core", "y", "x", "z")
            self.hops = [hops[name] for name in order]
            self.offsets, self.sizes = [0], [ch]
            for hop in self.hops:
                self.sizes.append(self.sizes[-1] // hop.size)
                self.offsets.append(self.offsets[-1] + hop.place * self.sizes[-1])
            self.flying = None

        def rows(self, offset, count):
            return pl.ds(pl.multiple_of(offset, 8), count)

        def sems(self, kind, level, step):
            before = sum(hop.size - 1 for hop in self.hops[:level]) + step - 1
            return ref[kind + "_send"].at[self.tap, before], ref[kind + "_recv"].at[self.tap, before]

        def scatter(self, level):
            hop, size = self.hops[level], self.sizes[level + 1]
            self.flying = []
            for step in range(1, hop.size):
                peer = lax.rem(hop.place + step, hop.size)
                send, recv = self.sems("rs", level, step)
                copy = pltpu.make_async_remote_copy(
                    src_ref=part_ref.at[self.tap, self.rows(self.offsets[level] + peer * size, size), :],
                    dst_ref=ref[f"land{level}"].at[self.tap, pl.ds((step - 1) * size, size), :],
                    send_sem=send,
                    recv_sem=recv,
                    device_id=hop.target(peer),
                    device_id_type=MESH,
                )
                copy.start()
                self.flying.append(copy)

        def gather(self, level):
            hop, size = self.hops[level], self.sizes[level + 1]
            mine = whole.at[self.tap, self.rows(self.offsets[level + 1], size), :]
            self.flying = []
            for step in range(1, hop.size):
                peer = lax.rem(hop.place + step, hop.size)
                send, recv = self.sems("ag", level, step)
                copy = pltpu.make_async_remote_copy(
                    src_ref=mine, dst_ref=mine, send_sem=send, recv_sem=recv,
                    device_id=hop.target(peer), device_id_type=MESH,
                )
                copy.start()
                self.flying.append(copy)

        def step(self, number):
            count = len(self.hops)
            if number == 0:
                part_ref[self.tap] = weight_grad(self.tap)
                self.scatter(0)
            elif number <= count:
                for copy in self.flying:
                    copy.wait()
                size = self.sizes[number]
                where = self.rows(self.offsets[number], size)
                total = part_ref[self.tap, where, :]
                for slot in range(self.hops[number - 1].size - 1):
                    total = total + ref[f"land{number - 1}"][self.tap, slot * size : (slot + 1) * size, :]
                if number < count:
                    part_ref[self.tap, where, :] = total
                    self.scatter(number)
                else:
                    whole[self.tap, where, :] = total
                    self.gather(count - 1)
            else:
                for copy in self.flying:
                    copy.wait()
                if number < 2 * count:
                    self.gather(2 * count - 1 - number)

    chunks = [Chunk(tap) for tap in range(9)]
    for tap in range(9 + 2):
        if tap < 9:
            chunks[tap].step(0)
        if tap >= 2:
            chunks[tap - 2].step(1)
    last = 2 * 4
    for wave in range(9 + last):
        if jobs:
            jobs.pop(0)()
        for tap in range(9):
            number = 2 + wave - tap
            if 2 <= number <= last:
                chunks[tap].step(number)
    for job in jobs:
        job()


def shards(mesh_shape, *arrays):
    feats, cots = arrays[0:4], arrays[4:8]
    weight, gain, shift, heights, widths = arrays[8:13]
    wide, group = mesh_shape["wide"], mesh_shape["group"]
    extents = tuple(feat.shape[1] for feat in feats)
    ch = weight.shape[3]
    devices = wide * group
    y_size = max(group // 2, 1)
    x_size = math.gcd(y_size, wide)
    z_size = wide // x_size
    fused = group == 2 * y_size and ch % (8 * devices) == 0
    segments, places, total_rows = plan(extents)
    levels = len(extents)
    vmem = pl.BlockSpec(memory_space=pltpu.VMEM)
    smem = pl.BlockSpec(memory_space=pltpu.SMEM)

    names, ins = [], []

    def give(name, array, spec):
        names.append(name)
        ins.append((array, spec))

    for index in range(levels):
        give(f"feat{index}", feats[index], vmem)
    for index in range(levels):
        give(f"grad{index}", cots[index], vmem)
    give("weight", weight, vmem)
    give("gain", gain, vmem)
    give("shift", shift, vmem)
    give("heights", heights, smem)
    give("widths", widths, smem)

    outs = []
    for index in range(levels):
        names.append(f"out{index}")
        outs.append(jax.ShapeDtypeStruct(feats[index].shape, jnp.bfloat16))
    for index in range(levels):
        names.append(f"d_feat{index}")
        outs.append(jax.ShapeDtypeStruct(feats[index].shape, jnp.bfloat16))
    names.append("d_weight")
    outs.append(jax.ShapeDtypeStruct((9, ch, ch), jnp.float32))
    for name in ("d_gain", "d_shift"):
        names.append(name)
        outs.append(jax.ShapeDtypeStruct((levels, ch), jnp.float32))

    scratch = []

    def hold(name, kind):
        names.append(name)
        scratch.append(kind)

    f32 = jnp.float32
    for number, segment in enumerate(segments):
        tall = segment["rows"] + 2 * segment["pitch"]
        hold(f"xb{number}", pltpu.VMEM((tall, 3 * ch), jnp.bfloat16))
        hold(f"bb{number}", pltpu.VMEM((tall, 3 * ch), jnp.bfloat16))
    for index in range(levels):
        hold(f"stage{index}", pltpu.VMEM((extents[index], places[index][3], ch), f32))
    for name in ("masks", "conv", "grads", "acts"):
        hold(name, pltpu.VMEM((total_rows, ch), f32))
    hold("turned", pltpu.VMEM((ch, total_rows), jnp.bfloat16))
    for tag, across in (("1", ch + 128), ("2", ch)):
        hold("sums" + tag, pltpu.VMEM((2 * levels, across), f32))
        hold("held" + tag, pltpu.VMEM((2 * levels, across), f32))
        hold("near" + tag, pltpu.VMEM((group, 2 * levels, across), f32))
        hold("far" + tag, pltpu.VMEM((wide, 2 * levels, across), f32))
        for name, size in (("near", group), ("far", wide)):
            hold(f"{name}_send{tag}", pltpu.SemaphoreType.DMA((max(size - 1, 1),)))
            hold(f"{name}_recv{tag}", pltpu.SemaphoreType.DMA((max(size - 1, 1),)))
    if fused:
        hold("parts", pltpu.VMEM((9, ch, ch), f32))
        hold("land0", pltpu.VMEM((9, ch // 2, ch), f32))
        across = x_size
        rows = ch // 2
        hold("land1", pltpu.VMEM((9, rows // x_size * (x_size - 1), ch), f32))
        rows //= x_size
        hold("land2", pltpu.VMEM((9, rows // y_size * (y_size - 1), ch), f32))
        rows //= y_size
        hold("land3", pltpu.VMEM((9, rows // z_size * (z_size - 1), ch), f32))
        flights = 1 + x_size - 1 + y_size - 1 + z_size - 1
        for name in ("rs_send", "rs_recv", "ag_send", "ag_recv"):
            hold(name, pltpu.SemaphoreType.DMA((9, flights)))

    shape = dict(
        names=names, extents=extents, wide=wide, group=group, ch=ch,
        x=x_size, y=y_size, z=z_size, fused=fused,
    )
    results = pl.pallas_call(
        functools.partial(kernel, shape),
        out_shape=outs,
        in_specs=[spec for _, spec in ins],
        out_specs=[vmem] * len(outs),
        scratch_shapes=scratch,
        compiler_params=pltpu.CompilerParams(
            collective_id=0, has_side_effects=True, vmem_limit_bytes=58 * 1024 * 1024
        ),
    )(*[array for array, _ in ins])
    results = list(results)
    d_weight = results[2 * levels]
    if not fused:
        d_weight = lax.psum(d_weight, ("wide", "group"))
    results[2 * levels] = (d_weight / devices).reshape(weight.shape)
    return tuple(results)


def solution(mesh):
    image = P(("wide", "group"), None, None, None)
    return jax.shard_map(
        functools.partial(shards, dict(mesh.shape)),
        mesh=mesh,
        in_specs=(image,) * 8 + (P(),) * 3 + (P(("wide", "group")),) * 2,
        out_specs=(image,) * 8 + (P(),) * 3,
        check_vma=False,
    )
```

time: 301 us -> 95.2 us (0.32)
  waiting for transfers between devices: 127 us -> 0 us
  Pallas kernels: 0 us -> 83.3 us
  blocking collectives: 54.4 us -> 0 us
  other arithmetic: 41.2 us -> 3.36 us
  matrix products: 34 us -> 0 us
  local copies, waits for them, and re-layouts: 24.6 us -> 6.34 us
  between operations: 18.1 us -> 2.04 us
    psum x2 -> x0, waiting for transfers between devices: 127 us -> none  [the longest x1 106 us: combine_grads(): result = lax.psum(within, 'wide')]
    pallas_call x0 -> x1, Pallas kernels: none -> 83.3 us  [shards(): pl.pallas_call(functools.partial(kernel, shape), out_shape=outs, in_specs...]
    psum x4 -> x0, blocking collectives: 54.4 us -> none  [the longest x2 39.7 us: combine_stats(): result = lax.psum(within, 'wide')]
    dot_general x108 -> x0, matrix products: 34 us -> none  [the longest x36 14.1 us: input_grad_rows(): lax.dot_general(window.reshape(row_count * extent, -1), conv_weight[tap_r...]
    reshape x57 -> x0, local copies, waits for them, and re-layouts: 14.8 us -> none  [the longest x24 11.1 us: input_grad_rows(): window.reshape(row_count * extent, -1)]
    div x7 -> x1, other arithmetic: 15 us -> 3.36 us  [shards(): results[2 * levels] = (d_weight / devices).reshape(weight.shape)]
    convert_element_type x17 -> x0, other arithmetic: 11.3 us -> none  [the longest x4 4.99 us: shards(): input_grads.append((weighted * input_part).astype(jnp.bfloat16)[None])]
    mul x12 -> x0, other arithmetic: 5.96 us -> none  [the longest x8 3.62 us: shards(): feature * weighted.astype(feature.dtype)]
  transfers between devices with their start and end apart: 2 -> 0, of which waited for: 2 -> 0; matrix products, arithmetic and copies ran while one was open for 12% -> 0% of each run, Pallas kernels for 0% -> 0%
where the time goes in v1:
time: 95.2 us; the launch traced here: 95 us
  Pallas kernels  83.3 us (88%)
  local copies, waits for them, and re-layouts  6.34 us (7%)
  other arithmetic  3.36 us (4%)
  between operations  2.04 us (2%)
    pallas_call x1, Pallas kernels, shards(): pl.pallas_call(functools.partial(kernel, shape), out_shape=outs, in_specs...  83.3 us
    unnamed x30, local copies, waits for them, and re-layouts  6.34 us
    div x1, other arithmetic, shards(): results[2 * levels] = (d_weight / devices).reshape(weight.shape)  3.36 us

profile of v1, /device:TPU:0, one launch (start us, length us, event | category | flops | bytes accessed | tf_op | source)
XLA Modules:
  0.0 95.0 jit_solution(3897877385362173046)
XLA Ops:
  1.9 83.3 %shard_map.212 = (bf16[1,24,24,256]{3,2,1,0:T(8,128)(2,1)}, bf16[1,12,12,256]{3,2,1,0:T(8,128)(2,1)}, bf16[1,6,6,256]{3,2,1,0:T(8,128)(2,1)}, bf16[1,3,3,256]{3,...) custom-call(bf16[1,24,24,256]{3,2,1,0:T(8,128)(2,1)} %refs_0_.1, ...), custom_call_target="tpu_custom_call" | custom-call | tf_op jit(solution)/shard_map/pallas_call | solution.py:501
  85.2 0.0 copy-start.1
  85.2 0.0 copy-start.3
  85.2 0.0 copy-start.5
  85.2 0.0 copy-start.7
  85.3 0.0 copy-start
  85.3 0.0 copy-start.2
  85.3 0.0 copy-start.4
  85.3 0.0 copy-start.6
  85.3 0.0 copy-start.9
  85.3 0.0 copy-start.8
  85.3 3.4 %broadcast_multiply_fusion = f32[9,256,256]{2,1,0:T(8,128)} fusion(f32[9,256,256]{2,1,0:T(8,128)} %get-tuple-element.30), kind=kLoop, calls=%fused_computation | loop fusion | flops 589824 | bytes 4718592 | tf_op jit(solution)/shard_map/div | solution.py:515
  88.7 0.7 copy.36
  89.4 0.6 copy.37
  90.0 0.6 copy.38
  90.7 0.6 copy.39
  91.2 0.7 copy.40
  92.0 0.6 copy.41
  92.6 0.6 copy.42
  93.2 0.0 copy-done.6
  93.2 0.6 copy.43
  93.8 0.0 copy-done.9
  93.8 0.6 copy.44
  94.4 0.6 copy.45
  (8 shorter events, 0.0 us)
Async XLA Ops:
  85.2 3.5 %copy-start.1 = (bf16[1,24,24,256]{3,2,1,0:T(8,128)(2,1)S(1)}, bf16[1,24,24,256]{3,2,1,0:T(8,128)(2,1)}, u32[]{:S(2)}) copy-start(bf16[1,24,24,256]{3,2,1,0:T(8,128)(2,1)} %get-tuple-element.44) | copy-start | bytes 884740
  85.2 4.2 %copy-start.3 = (bf16[1,12,12,256]{3,2,1,0:T(8,128)(2,1)S(1)}, bf16[1,12,12,256]{3,2,1,0:T(8,128)(2,1)}, u32[]{:S(2)}) copy-start(bf16[1,12,12,256]{3,2,1,0:T(8,128)(2,1)} %get-tuple-element.45) | copy-start | bytes 221188
  85.2 4.8 %copy-start.5 = (bf16[1,6,6,256]{3,2,1,0:T(8,128)(2,1)S(1)}, bf16[1,6,6,256]{3,2,1,0:T(8,128)(2,1)}, u32[]{:S(2)}) copy-start(bf16[1,6,6,256]{3,2,1,0:T(8,128)(2,1)} %get-tuple-element.46) | copy-start | bytes 55300
  85.2 5.4 %copy-start.7 = (bf16[1,3,3,256]{3,2,1,0:T(4,128)(2,1)S(1)}, bf16[1,3,3,256]{3,2,1,0:T(4,128)(2,1)}, u32[]{:S(2)}) copy-start(bf16[1,3,3,256]{3,2,1,0:T(4,128)(2,1)} %get-tuple-element.47) | copy-start | bytes 13828
  85.3 6.0 %copy-start = (bf16[1,24,24,256]{3,2,1,0:T(8,128)(2,1)S(1)}, bf16[1,24,24,256]{3,2,1,0:T(8,128)(2,1)}, u32[]{:S(2)}) copy-start(bf16[1,24,24,256]{3,2,1,0:T(8,128)(2,1)} %get-tuple-element.48) | copy-start | bytes 884740
  85.3 6.7 %copy-start.2 = (bf16[1,12,12,256]{3,2,1,0:T(8,128)(2,1)S(1)}, bf16[1,12,12,256]{3,2,1,0:T(8,128)(2,1)}, u32[]{:S(2)}) copy-start(bf16[1,12,12,256]{3,2,1,0:T(8,128)(2,1)} %get-tuple-element.49) | copy-start | bytes 221188
  85.3 7.3 %copy-start.4 = (bf16[1,6,6,256]{3,2,1,0:T(8,128)(2,1)S(1)}, bf16[1,6,6,256]{3,2,1,0:T(8,128)(2,1)}, u32[]{:S(2)}) copy-start(bf16[1,6,6,256]{3,2,1,0:T(8,128)(2,1)} %get-tuple-element.50) | copy-start | bytes 55300
  85.3 7.9 %copy-start.6 = (bf16[1,3,3,256]{3,2,1,0:T(4,128)(2,1)S(1)}, bf16[1,3,3,256]{3,2,1,0:T(4,128)(2,1)}, u32[]{:S(2)}) copy-start(bf16[1,3,3,256]{3,2,1,0:T(4,128)(2,1)} %get-tuple-element.51) | copy-start | bytes 13828
  85.3 8.5 %copy-start.9 = (f32[4,256]{1,0:T(4,128)S(1)}, f32[4,256]{1,0:T(4,128)}, u32[]{:S(2)}) copy-start(f32[4,256]{1,0:T(4,128)} %get-tuple-element.53) | copy-start | bytes 12292
  85.3 9.1 %copy-start.8 = (f32[4,256]{1,0:T(4,128)S(1)}, f32[4,256]{1,0:T(4,128)}, u32[]{:S(2)}) copy-start(f32[4,256]{1,0:T(4,128)} %get-tuple-element.54) | copy-start | bytes 12292

commit v2 on v1

--- a/solution.py
+++ b/solution.py
@@ -11,6 +11,7 @@
 EPSILON = 1e-05
 MESH = pl.DeviceIdType.MESH
 TILE = 48
+SKEW = 3
 
 
 def plan(extents):
@@ -385,7 +386,7 @@
                     part_ref[self.tap, where, :] = total
                     self.scatter(number)
                 else:
-                    whole[self.tap, where, :] = total
+                    whole[self.tap, where, :] = total / devices
                     self.gather(count - 1)
             else:
                 for copy in self.flying:
@@ -399,16 +400,40 @@
             chunks[tap].step(0)
         if tap >= 2:
             chunks[tap - 2].step(1)
-    last = 2 * 4
-    for wave in range(9 + last):
-        if jobs:
+    turns = [(tap + SKEW * number, -number, tap) for tap in range(9) for number in range(2, 9)]
+    for place, (_, number, tap) in enumerate(sorted(turns)):
+        if jobs and place % 2 == 0:
             jobs.pop(0)()
-        for tap in range(9):
-            number = 2 + wave - tap
-            if 2 <= number <= last:
-                chunks[tap].step(number)
-    for job in jobs:
-        job()
+        chunks[tap].step(-number)
+
+
+def hand_on(arrays):
+    count = len(arrays)
+
+    def body(*refs):
+        sources, targets, held = refs[:count], refs[count : 2 * count], refs[2 * count : 3 * count]
+        read, write = refs[3 * count :]
+        reads = [pltpu.make_async_copy(sources[i], held[i], read.at[i]) for i in range(count)]
+        writes = [pltpu.make_async_copy(held[i], targets[i], write.at[i]) for i in range(count)]
+        for copy in reads:
+            copy.start()
+        for first, second in zip(reads, writes):
+            first.wait()
+            second.start()
+        for copy in writes:
+            copy.wait()
+
+    return list(
+        pl.pallas_call(
+            body,
+            out_shape=[jax.ShapeDtypeStruct(array.shape, array.dtype) for array in arrays],
+            in_specs=[pl.BlockSpec(memory_space=pl.ANY)] * count,
+            out_specs=[pl.BlockSpec(memory_space=pl.ANY)] * count,
+            scratch_shapes=[pltpu.VMEM(array.shape, array.dtype) for array in arrays]
+            + [pltpu.SemaphoreType.DMA((count,))] * 2,
+            compiler_params=pltpu.CompilerParams(vmem_limit_bytes=8 * 1024 * 1024),
+        )(*arrays)
+    )
 
 
 def shards(mesh_shape, *arrays):
@@ -505,14 +530,17 @@
         out_specs=[vmem] * len(outs),
         scratch_shapes=scratch,
         compiler_params=pltpu.CompilerParams(
-            collective_id=0, has_side_effects=True, vmem_limit_bytes=58 * 1024 * 1024
+            collective_id=0, has_side_effects=True, vmem_limit_bytes=32 * 1024 * 1024
         ),
     )(*[array for array, _ in ins])
     results = list(results)
-    d_weight = results[2 * levels]
-    if not fused:
-        d_weight = lax.psum(d_weight, ("wide", "group"))
-    results[2 * levels] = (d_weight / devices).reshape(weight.shape)
+    d_weight = results.pop(2 * levels)
+    if fused:
+        *results, d_weight = hand_on(results + [d_weight])
+    else:
+        results = hand_on(results)
+        d_weight = lax.psum(d_weight, ("wide", "group")) / devices
+    results.insert(2 * levels, d_weight.reshape(weight.shape))
     return tuple(results)
 
 

time: 95.2 us -> 73.6 us (0.77)
  Pallas kernels: 83.3 us -> 61.9 us
  other arithmetic: 3.36 us -> 0 us
  local copies, waits for them, and re-layouts: 6.34 us -> 9.2 us
    pallas_call x1, Pallas kernels: 83.3 us -> 59.3 us  [shards(): pl.pallas_call(functools.partial(kernel, shape), out_shape=outs, in_specs...]
    div x1 -> x0, other arithmetic: 3.36 us -> none  [shards(): results[2 * levels] = (d_weight / devices).reshape(weight.shape)]
    unnamed x30 -> x22, local copies, waits for them, and re-layouts: 6.34 us -> 9.2 us
    pallas_call x0 -> x1, Pallas kernels: none -> 2.6 us  [hand_on(): pl.pallas_call(body, out_shape=[jax.ShapeDtypeStruct(array.shape, array.d...]
where the time goes in v2:
time: 73.6 us; the launch traced here: 73 us
  Pallas kernels  61.9 us (84%)
  local copies, waits for them, and re-layouts  9.2 us (12%)
  between operations  1.97 us (3%)
    pallas_call x1, Pallas kernels, shards(): pl.pallas_call(functools.partial(kernel, shape), out_shape=outs, in_specs...  59.3 us
    unnamed x22, local copies, waits for them, and re-layouts  9.2 us
    pallas_call x1, Pallas kernels, hand_on(): pl.pallas_call(body, out_shape=[jax.ShapeDtypeStruct(array.shape, array.d...  2.6 us

profile of v2, /device:TPU:0, one launch (start us, length us, event | category | flops | bytes accessed | tf_op | source)
XLA Modules:
  0.0 73.0 jit_solution(3814763117851248164)
XLA Ops:
  1.9 0.0 copy-start
  1.9 1.3 %copy-done = bf16[3,3,256,256]{3,2,1,0:T(8,128)(2,1)S(1)} copy-done((bf16[3,3,256,256]{3,2,1,0:T(8,128)(2,1)S(1)}, bf16[3,3,256,256]{3,2,1,0:T(8,128)(2,1)}, u32[]{:S(2)}) %copy-start) | copy-done | bytes 1179672
  3.2 0.0 copy-start.1
  3.2 1.0 %copy-done.1 = bf16[1,24,24,256]{3,2,1,0:T(8,128)(2,1)S(1)} copy-done((bf16[1,24,24,256]{3,2,1,0:T(8,128)(2,1)S(1)}, bf16[1,24,24,256]{3,2,1,0:T(8,128)(2,1)}, u32[]{:S(2)}) %copy-start.1) | copy-done | bytes 294936
  4.2 0.0 copy-start.2
  4.2 1.0 %copy-done.2 = bf16[1,24,24,256]{3,2,1,0:T(8,128)(2,1)S(1)} copy-done((bf16[1,24,24,256]{3,2,1,0:T(8,128)(2,1)S(1)}, bf16[1,24,24,256]{3,2,1,0:T(8,128)(2,1)}, u32[]{:S(2)}) %copy-start.2) | copy-done | bytes 294936
  5.1 0.0 copy-start.3
  5.1 0.9 %copy-done.3 = bf16[1,12,12,256]{3,2,1,0:T(8,128)(2,1)S(1)} copy-done((bf16[1,12,12,256]{3,2,1,0:T(8,128)(2,1)S(1)}, bf16[1,12,12,256]{3,2,1,0:T(8,128)(2,1)}, u32[]{:S(2)}) %copy-start.3) | copy-done | bytes 73752
  6.0 0.0 copy-start.4
  6.0 0.9 %copy-done.4 = bf16[1,12,12,256]{3,2,1,0:T(8,128)(2,1)S(1)} copy-done((bf16[1,12,12,256]{3,2,1,0:T(8,128)(2,1)S(1)}, bf16[1,12,12,256]{3,2,1,0:T(8,128)(2,1)}, u32[]{:S(2)}) %copy-start.4) | copy-done | bytes 73752
  6.9 0.0 copy-start.5
  6.9 0.7 %copy-done.5 = bf16[1,6,6,256]{3,2,1,0:T(8,128)(2,1)S(1)} copy-done((bf16[1,6,6,256]{3,2,1,0:T(8,128)(2,1)S(1)}, bf16[1,6,6,256]{3,2,1,0:T(8,128)(2,1)}, u32[]{:S(2)}) %copy-start.5) | copy-done | bytes 18456
  7.7 0.0 copy-start.6
  7.7 0.7 %copy-done.6 = bf16[1,6,6,256]{3,2,1,0:T(8,128)(2,1)S(1)} copy-done((bf16[1,6,6,256]{3,2,1,0:T(8,128)(2,1)S(1)}, bf16[1,6,6,256]{3,2,1,0:T(8,128)(2,1)}, u32[]{:S(2)}) %copy-start.6) | copy-done | bytes 18456
  8.4 0.0 copy-start.7
  8.4 0.7 copy-done.7
  9.1 0.0 copy-start.8
  9.1 0.7 copy-done.8
  9.8 0.0 copy-start.9
  9.8 0.7 copy-done.9
  10.5 0.0 copy-start.10
  10.5 0.7 copy-done.10
  11.2 59.3 %shard_map.212 = (bf16[1,24,24,256]{3,2,1,0:T(8,128)(2,1)S(1)}, bf16[1,12,12,256]{3,2,1,0:T(8,128)(2,1)S(1)}, bf16[1,6,6,256]{3,2,1,0:T(8,128)(2,1)S(1)}, bf16[1...) custom-call(bf16[1,24,24,256]{3,2,1,0:T(8,128)(2,1)S(1)} %copy-done., ...), custom_call_target="tpu_custom_call" | custom-call | tf_op jit(solution)/shard_map/pallas_call | solution.py:526
  70.4 2.6 %shard_map.213 = (bf16[1,24,24,256]{3,2,1,0:T(8,128)(2,1)}, bf16[1,12,12,256]{3,2,1,0:T(8,128)(2,1)}, bf16[1,6,6,256]{3,2,1,0:T(8,128)(2,1)}, bf16[1,3,3,256]{3,...) custom-call(bf16[1,24,24,256]{3,2,1,0:T(8,128)(2,1)S(1)} %get-tuple-, ...), custom_call_target="tpu_custom_call" | custom-call | tf_op jit(solution)/shard_map/pallas_call | solution.py:427
Async XLA Ops:
  1.9 1.3 %copy-start = (bf16[3,3,256,256]{3,2,1,0:T(8,128)(2,1)S(1)}, bf16[3,3,256,256]{3,2,1,0:T(8,128)(2,1)}, u32[]{:S(2)}) copy-start(bf16[3,3,256,256]{3,2,1,0:T(8,128)(2,1)} %refs_8_.1) | copy-start | bytes 3538948
  3.2 1.0 %copy-start.1 = (bf16[1,24,24,256]{3,2,1,0:T(8,128)(2,1)S(1)}, bf16[1,24,24,256]{3,2,1,0:T(8,128)(2,1)}, u32[]{:S(2)}) copy-start(bf16[1,24,24,256]{3,2,1,0:T(8,128)(2,1)} %refs_0_.1) | copy-start | bytes 884740
  4.2 1.0 %copy-start.2 = (bf16[1,24,24,256]{3,2,1,0:T(8,128)(2,1)S(1)}, bf16[1,24,24,256]{3,2,1,0:T(8,128)(2,1)}, u32[]{:S(2)}) copy-start(bf16[1,24,24,256]{3,2,1,0:T(8,128)(2,1)} %refs_4_.1) | copy-start | bytes 884740
  5.1 0.9 %copy-start.3 = (bf16[1,12,12,256]{3,2,1,0:T(8,128)(2,1)S(1)}, bf16[1,12,12,256]{3,2,1,0:T(8,128)(2,1)}, u32[]{:S(2)}) copy-start(bf16[1,12,12,256]{3,2,1,0:T(8,128)(2,1)} %refs_1_.1) | copy-start | bytes 221188
  6.0 0.9 %copy-start.4 = (bf16[1,12,12,256]{3,2,1,0:T(8,128)(2,1)S(1)}, bf16[1,12,12,256]{3,2,1,0:T(8,128)(2,1)}, u32[]{:S(2)}) copy-start(bf16[1,12,12,256]{3,2,1,0:T(8,128)(2,1)} %refs_5_.1) | copy-start | bytes 221188
  6.9 0.7 %copy-start.5 = (bf16[1,6,6,256]{3,2,1,0:T(8,128)(2,1)S(1)}, bf16[1,6,6,256]{3,2,1,0:T(8,128)(2,1)}, u32[]{:S(2)}) copy-start(bf16[1,6,6,256]{3,2,1,0:T(8,128)(2,1)} %refs_2_.1) | copy-start | bytes 55300
  7.7 0.7 %copy-start.6 = (bf16[1,6,6,256]{3,2,1,0:T(8,128)(2,1)S(1)}, bf16[1,6,6,256]{3,2,1,0:T(8,128)(2,1)}, u32[]{:S(2)}) copy-start(bf16[1,6,6,256]{3,2,1,0:T(8,128)(2,1)} %refs_6_.1) | copy-start | bytes 55300
  8.4 0.7 copy-start.7
  9.1 0.7 copy-start.8
  9.8 0.7 copy-start.9
  10.5 0.7 copy-start.10

commit v3 on v2

--- a/solution.py
+++ b/solution.py
@@ -63,6 +63,15 @@
     def at_wide(w):
         return {"wide": w, "group": g_me}
 
+    loads = {}
+    for number, name in enumerate(shape["loaded"]):
+        loads[name] = pltpu.make_async_copy(ref[name], ref["vmem_" + name], ref["load"].at[number])
+        loads[name].start()
+        ref[name] = ref["vmem_" + name]
+    stores = {}
+    for number, name in enumerate(shape["stored"]):
+        stores[name] = pltpu.make_async_copy(ref["vmem_" + name], ref[name], ref["store"].at[number])
+        ref[name] = ref["vmem_" + name]
     barrier = pltpu.get_barrier_semaphore()
     for step in range(1, group):
         pl.semaphore_signal(barrier, inc=1, device_id=at_group(lax.rem(g_me + step, group)), device_id_type=MESH)
@@ -107,9 +116,11 @@
         masks[start : start + size, :] = mask
         stage = ref[f"stage{index}"]
         stage[...] = jnp.zeros(stage.shape, jnp.float32)
+        loads[f"feat{index}"].wait()
         stage[:, 0:extent, :] = ref[f"feat{index}"][0].astype(jnp.float32)
         spread(xbs, index, stage[...].reshape(size, ch) * mask)
 
+    loads["weight"].wait()
     weight = ref["weight"]
     sums = ref["sums1"]
 
@@ -198,6 +209,7 @@
             start, size = span(index)
             extent = extents[index]
             stage = ref[f"stage{index}"]
+            loads[f"grad{index}"].wait()
             stage[:, 0:extent, :] = ref[f"grad{index}"][0].astype(jnp.float32)
             grads[start : start + size, :] = stage[...].reshape(size, ch) * masks[start : start + size, :]
 
@@ -209,6 +221,8 @@
                 ref["turned"][:, base + row : base + row + 128] = block.astype(jnp.float32).T.astype(jnp.bfloat16)
 
     moments = exchange("1", (take_grads, turn))
+    loads["gain"].wait()
+    loads["shift"].wait()
 
     sums = ref["sums2"]
     scales, counts = [], []
@@ -243,10 +257,13 @@
             extent, pitch = extents[index], places[index][3]
             values = ref["acts"][start : start + size, :].reshape(extent, pitch, ch)
             ref[f"out{index}"][0] = values[:, 0:extent, :].astype(jnp.bfloat16)
+            stores[f"out{index}"].start()
 
     slopes = exchange("2", (lambda: None, put_acts))
     ref["d_shift"][...] = slopes[0:levels, :] / devices
     ref["d_gain"][...] = slopes[levels : 2 * levels, :] / devices
+    stores["d_shift"].start()
+    stores["d_gain"].start()
 
     for index in range(levels):
         start, size = span(index)
@@ -295,6 +312,7 @@
             extent, pitch = extents[index], places[index][3]
             values = ref["acts"][start : start + size, :].reshape(extent, pitch, ch)
             ref[f"d_feat{index}"][0] = values[:, 0:extent, :].astype(jnp.bfloat16)
+            stores[f"d_feat{index}"].start()
 
     jobs = []
     for number, segment in enumerate(segments):
@@ -308,6 +326,9 @@
             ref["d_weight"][tap] = weight_grad(tap)
         for job in jobs:
             job()
+        stores["d_weight"].start()
+        for copy in stores.values():
+            copy.wait()
         return
 
     part_ref, whole = ref["parts"], ref["d_weight"]
@@ -405,6 +426,9 @@
         if jobs and place % 2 == 0:
             jobs.pop(0)()
         chunks[tap].step(-number)
+    stores["d_weight"].start()
+    for copy in stores.values():
+        copy.wait()
 
 
 def hand_on(arrays):
@@ -431,7 +455,7 @@
             out_specs=[pl.BlockSpec(memory_space=pl.ANY)] * count,
             scratch_shapes=[pltpu.VMEM(array.shape, array.dtype) for array in arrays]
             + [pltpu.SemaphoreType.DMA((count,))] * 2,
-            compiler_params=pltpu.CompilerParams(vmem_limit_bytes=8 * 1024 * 1024),
+            compiler_params=pltpu.CompilerParams(vmem_limit_bytes=58 * 1024 * 1024),
         )(*arrays)
     )
 
@@ -449,7 +473,6 @@
     fused = group == 2 * y_size and ch % (8 * devices) == 0
     segments, places, total_rows = plan(extents)
     levels = len(extents)
-    vmem = pl.BlockSpec(memory_space=pltpu.VMEM)
     smem = pl.BlockSpec(memory_space=pltpu.SMEM)
 
     names, ins = [], []
@@ -458,13 +481,15 @@
         names.append(name)
         ins.append((array, spec))
 
-    for index in range(levels):
-        give(f"feat{index}", feats[index], vmem)
-    for index in range(levels):
-        give(f"grad{index}", cots[index], vmem)
-    give("weight", weight, vmem)
-    give("gain", gain, vmem)
-    give("shift", shift, vmem)
+    hbm = pl.BlockSpec(memory_space=pltpu.HBM)
+    for index in range(levels):
+        give(f"feat{index}", feats[index], hbm)
+    give("weight", weight, hbm)
+    for index in range(levels):
+        give(f"grad{index}", cots[index], hbm)
+    give("gain", gain, hbm)
+    give("shift", shift, hbm)
+    loaded = tuple(names)
     give("heights", heights, smem)
     give("widths", widths, smem)
 
@@ -482,12 +507,19 @@
         outs.append(jax.ShapeDtypeStruct((levels, ch), jnp.float32))
 
     scratch = []
+    stored = tuple(names[len(ins) :])
 
     def hold(name, kind):
         names.append(name)
         scratch.append(kind)
 
     f32 = jnp.float32
+    for name, (array, _) in zip(loaded, ins):
+        hold("vmem_" + name, pltpu.VMEM(array.shape, array.dtype))
+    for name, out in zip(stored, outs):
+        hold("vmem_" + name, pltpu.VMEM(out.shape, out.dtype))
+    hold("store", pltpu.SemaphoreType.DMA((len(stored),)))
+    hold("load", pltpu.SemaphoreType.DMA((len(loaded),)))
     for number, segment in enumerate(segments):
         tall = segment["rows"] + 2 * segment["pitch"]
         hold(f"xb{number}", pltpu.VMEM((tall, 3 * ch), jnp.bfloat16))
@@ -521,16 +553,16 @@
 
     shape = dict(
         names=names, extents=extents, wide=wide, group=group, ch=ch,
-        x=x_size, y=y_size, z=z_size, fused=fused,
+        x=x_size, y=y_size, z=z_size, fused=fused, loaded=loaded, stored=stored,
     )
     results = pl.pallas_call(
         functools.partial(kernel, shape),
         out_shape=outs,
         in_specs=[spec for _, spec in ins],
-        out_specs=[vmem] * len(outs),
+        out_specs=[hbm] * len(outs),
         scratch_shapes=scratch,
         compiler_params=pltpu.CompilerParams(
-            collective_id=0, has_side_effects=True, vmem_limit_bytes=32 * 1024 * 1024
+            collective_id=0, has_side_effects=True, vmem_limit_bytes=58 * 1024 * 1024
         ),
     )(*[array for array, _ in ins])
     results = list(results)

time: 73.6 us -> 68.1 us (0.925)
  local copies, waits for them, and re-layouts: 9.2 us -> 0 us
  Pallas kernels: 61.9 us -> 65.9 us
    unnamed x22 -> x0, local copies, waits for them, and re-layouts: 9.2 us -> none
    pallas_call x1, Pallas kernels: 59.3 us -> 62.2 us  [shards(): pl.pallas_call(functools.partial(kernel, shape), out_shape=outs, in_specs...]
    pallas_call x1, Pallas kernels: 2.6 us -> 3.77 us  [hand_on(): pl.pallas_call(body, out_shape=[jax.ShapeDtypeStruct(array.shape, array.d...]
where the time goes in v3:
time: 68.1 us; the launch traced here: 67.9 us
  Pallas kernels  65.9 us (97%)
  between operations  1.95 us (3%)
    pallas_call x1, Pallas kernels, shards(): pl.pallas_call(functools.partial(kernel, shape), out_shape=outs, in_specs...  62.2 us
    pallas_call x1, Pallas kernels, hand_on(): pl.pallas_call(body, out_shape=[jax.ShapeDtypeStruct(array.shape, array.d...  3.77 us

profile of v3, /device:TPU:0, one launch (start us, length us, event | category | flops | bytes accessed | tf_op | source)
XLA Modules:
  0.0 67.9 jit_solution(2426162192601051177)
XLA Ops:
  1.9 62.2 %shard_map.212 = (bf16[1,24,24,256]{3,2,1,0:T(8,128)(2,1)}, bf16[1,12,12,256]{3,2,1,0:T(8,128)(2,1)}, bf16[1,6,6,256]{3,2,1,0:T(8,128)(2,1)}, bf16[1,3,3,256]{3,...) custom-call(bf16[1,24,24,256]{3,2,1,0:T(8,128)(2,1)} %refs_0_.1, ...), custom_call_target="tpu_custom_call" | custom-call | tf_op jit(solution)/shard_map/pallas_call | solution.py:558
  64.1 3.8 %shard_map.213 = (bf16[1,24,24,256]{3,2,1,0:T(8,128)(2,1)}, bf16[1,12,12,256]{3,2,1,0:T(8,128)(2,1)}, bf16[1,6,6,256]{3,2,1,0:T(8,128)(2,1)}, bf16[1,3,3,256]{3,...) custom-call(bf16[1,24,24,256]{3,2,1,0:T(8,128)(2,1)} %get-tuple-elem, ...), custom_call_target="tpu_custom_call" | custom-call | tf_op jit(solution)/shard_map/pallas_call | solution.py:451
